TPU v7x, 256 devices: a whole 4x4x8 slice. The times are simulated.
256 devices in a mesh: seq: 32 (over y, z), tp: 8 (over x, core).
Axes of the slice: x: 4, y: 4, z: 8, core: 2. Of those that a mesh axis runs over, the one named last changes fastest.
Arguments:
- tokens: bfloat16 [24576, 2048], P('seq', 'tp'), may hold values from -20 to 20
- w_query: bfloat16 [2048, 2048], P(None, 'tp'), may hold values from -0.125 to 0.125
- w_key: bfloat16 [2048, 2048], P(None, 'tp'), may hold values from -0.125 to 0.125
- w_value: bfloat16 [2048, 2048], P(None, 'tp'), may hold values from -0.125 to 0.125
- head_gain: float32 [2048], P('tp'), may hold values from 0.5 to 1.5
- w_out: bfloat16 [2048, 2048], P('tp'), may hold values from -0.125 to 0.125
- norm_gain: float32 [2048], replicated, may hold values from 0.5 to 1.5
- w_gate: bfloat16 [2048, 8192], P('seq', 'tp'), may hold values from -0.125 to 0.125
- w_up: bfloat16 [2048, 8192], P('seq', 'tp'), may hold values from -0.125 to 0.125
- w_down: bfloat16 [8192, 2048], P('tp', 'seq'), may hold values from -0.0625 to 0.0625
Outputs:
- layer_out: bfloat16 [24576, 2048], P('seq', 'tp')
All inputs are finite; a program needn't handle non-finite values.
Results may differ from a plain program's by a relative error of at most 0.009.
Values may be sent and summed in bfloat16 or wider, within the bound.
No kernel may reach another device: no remote copies, remote signals or barrier semaphores. Data moves between devices by JAX's collectives and lax.ppermute only.
A program may use at most 128 MiB of HBM per device.

v0:
```python
import jax
import jax.numpy as jnp
from jax import lax
from jax.sharding import Mesh
from jax.sharding import PartitionSpec as P

HD = 128
SEQ = ("seq_0", "seq_1")


def nothing_yet(array, identity):
    return jnp.zeros_like(array) + jnp.asarray(identity, array.dtype)


def entering(array, axes, combine, identity):
    before = start = nothing_yet(array, identity)
    total = array
    for axis in reversed(axes):
        peers, position = (lax.axis_size(axis), lax.axis_index(axis))
        pieces = lax.all_gather(total.astype(jnp.bfloat16), axis)
        inside, total = (start, start)
        for k in range(peers):
            passed = k < position
            total = combine(total, pieces[k].astype(array.dtype))
            inside = jnp.where(passed, total, inside)
        before = combine(inside, before)
    return before


def in_one_piece(arrays, axis, dim, along):
    ends, at = ([], 0)
    for a in arrays[:-1]:
        at += a.shape[along]
        ends.append(at)
    both = jnp.concatenate(arrays, axis=along)
    return tuple(jnp.split(lax.all_gather(both, axis, axis=dim, tiled=True), ends, axis=along))


def split_up(array, dim, peers):
    shape = array.shape
    tiles = array.reshape(*shape[:dim], peers, shape[dim] // peers, *shape[dim + 1 :])
    return jnp.moveaxis(tiles, dim, 0)


def sum_at_owner(array, axis, dim):
    tiles = split_up(array, dim, lax.axis_size(axis))
    arrived = lax.all_to_all(tiles, axis, split_axis=0, concat_axis=0, tiled=True)
    return arrived.astype(jnp.float32).sum(axis=0)


def add_states(earlier, later):
    return earlier + later


def body(tokens, w_query, w_key, w_value, head_gain, w_out, norm_gain, w_gate, w_up, w_down):
    length = tokens.shape[0]
    width_here = tokens.shape[1]
    heads_here = w_query.shape[1] // HD
    features = lax.all_gather(tokens, "tp", axis=1, tiled=True)

    def project(weight):
        product = jnp.dot(features, weight, preferred_element_type=jnp.float32)
        return product.astype(jnp.bfloat16).reshape(length, heads_here, HD)

    query = project(w_query)
    keys_local = project(w_key)
    values_local = project(w_value)
    scores = jnp.einsum("ihd,jhd->hij", query, keys_local, preferred_element_type=jnp.float32)
    causal = jnp.arange(length)[:, None] >= jnp.arange(length)[None, :]
    scores = jnp.where(causal[None], scores, 0.0).astype(jnp.bfloat16)
    inside = jnp.einsum("hij,jhd->ihd", scores, values_local, preferred_element_type=jnp.float32)
    own_state = jnp.einsum(
        "jhd,jhe->hde", keys_local, values_local, preferred_element_type=jnp.float32
    )
    history = entering(own_state, SEQ, add_states, jnp.zeros_like(own_state))
    carried = jnp.einsum(
        "ihd,hde->ihe", query, history.astype(jnp.bfloat16), preferred_element_type=jnp.float32
    )
    mixed = inside + carried
    scale = lax.rsqrt(jnp.mean(mixed * mixed, axis=-1, keepdims=True) + 1e-06)
    normed = (mixed * scale * head_gain.reshape(heads_here, HD)).astype(jnp.bfloat16)
    normed = normed.reshape(length, heads_here * HD)
    partial_value = jnp.dot(normed, w_out, preferred_element_type=jnp.float32)
    own_column = lax.axis_index("tp") * width_here
    summed = lax.psum(partial_value.astype(jnp.bfloat16), "tp").astype(jnp.float32)
    resid_whole = features.astype(jnp.float32) + summed
    factor = lax.rsqrt(jnp.mean(resid_whole * resid_whole, axis=-1, keepdims=True) + 1e-05)
    ffn_in = (resid_whole * factor * norm_gain).astype(jnp.bfloat16)
    resid = lax.dynamic_slice_in_dim(resid_whole, own_column, width_here, 1)
    pieces = in_one_piece((w_gate, w_up), SEQ, 0, 1)
    gate_sum = jnp.dot(ffn_in, pieces[0], preferred_element_type=jnp.float32)
    upward_sum = jnp.dot(ffn_in, pieces[1], preferred_element_type=jnp.float32)
    hidden = (jax.nn.silu(gate_sum) * upward_sum).astype(jnp.bfloat16)
    terms = jnp.dot(
        hidden, lax.all_gather(w_down, SEQ, axis=1, tiled=True), preferred_element_type=jnp.float32
    )
    mlp_share = sum_at_owner(terms.astype(jnp.bfloat16), "tp", 1)
    return (resid + mlp_share).astype(jnp.bfloat16)


def solution(mesh):
    finer = Mesh(mesh.devices.reshape(4, 8, mesh.shape["tp"]), ("seq_0", "seq_1", "tp"))
    return jax.shard_map(
        body,
        mesh=finer,
        in_specs=(
            P(SEQ, "tp"),
            P(None, "tp"),
            P(None, "tp"),
            P(None, "tp"),
            P("tp"),
            P("tp", None),
            P(),
            P(SEQ, "tp"),
            P(SEQ, "tp"),
            P("tp", SEQ),
        ),
        out_specs=P(SEQ, "tp"),
        check_vma=False,
    )
```

profile of v0, /device:TPU:1, one launch (start us, length us, event | category | flops | bytes accessed | tf_op | source)
XLA Modules:
  0.0 356.1 jit_solution(3774338087254047791)
XLA Ops:
  7.4 0.7 all-gather.5.cloned.1.call-update
  8.3 39.5 %all-gather.5.cloned.1.call-done = bf16[768,2048]{1,0:T(8,128)(2,1)} async-done(((bf16[768,256]{1,0:T(8,128)(2,1)}), bf16[768,2048]{1,0:T(8,128)(2,1)}) %all-gather.5.cloned.1.call-update) | async-done | bytes 3145744 | tf_op jit(solution)/shard_map/all_gather | solution.py:59
  47.9 3.3 convolution_convert_fusion.2
  51.2 2.4 convolution_convert_fusion.4
  53.9 20.8 %all-gather = bf16[16,128,128]{2,1,0:T(8,128)(2,1)S(1)} all-gather(bf16[2,128,128]{2,1,0:T(8,128)(2,1)S(1)} %convolution_convert_fusion.5), channel_id=2, replica_groups=mesh['seq_0'=4,'seq_1'=8,'tp'=8] {'seq_1'}, dimensions={0}, use_global_device_ids=true | all-gather | bytes 589824 | tf_op jit(solution)/shard_map/all_gather | solution.py:20
  74.7 9.7 %all_gather.22 = bf16[4,2,128,128]{3,2,1,0:T(8,128)(2,1)S(1)} all-gather(bf16[1,2,128,128]{3,2,1,0:T(8,128)(2,1)S(1)} %fusion.28), channel_id=1, replica_groups=mesh['seq_0'=4,'seq_1'=8,'tp'=8] {'seq_0'}, dimensions={0}, use_global_device_ids=true | all-gather | bytes 327680 | tf_op jit(solution)/shard_map/all_gather | solution.py:20
  84.5 1.1 convolution_convert_fusion.3
  85.6 0.7 copy-done.7
  86.3 1.3 fusion.29
  87.6 2.9 multiply_reduce_fusion.1
  90.6 2.7 convolution_convert_fusion.1
  93.5 0.8 copy-done.2
  94.3 0.7 pad_maximum_fusion
  95.7 79.1 %all-reduce.2.cloned.1.call-done = bf16[768,2048]{1,0:T(8,128)(2,1)} async-done(((bf16[768,2048]{1,0:T(8,128)(2,1)}), bf16[768,2048]{1,0:T(8,128)(2,1)}) %all-reduce.2.cloned.1.call-update) | async-done | bytes 3145744 | tf_op jit(solution)/shard_map/psum | solution.py:85
  174.8 6.7 %convert_add_fusion = (f32[768,2048]{1,0:T(8,128)}, f32[768]{0:T(1024)S(1)}) fusion(bf16[768,2048]{1,0:T(8,128)(2,1)} %all-reduce.2.cloned.1.call-done, bf16[768,2048]{1,0:T(8,128)(2,1)} %all-gather.5.cloned.1.call-done), kind=kLoop, calls=%fused_computation.3 | loop fusion | flops 7863552 | bytes 12585984 | tf_op jit(solution)/shard_map/add | solution.py:86
  181.6 19.3 %all-gather.7.cloned.1.call-done = bf16[2048,2048]{1,0:T(8,128)(2,1)} async-done(((bf16[64,2048]{1,0:T(8,128)(2,1)}), bf16[2048,2048]{1,0:T(8,128)(2,1)}) %all-gather.7.cloned.1.call-update) | async-done | bytes 8388624 | tf_op jit(solution)/shard_map/all_gather | solution.py:36
  200.9 9.2 %fusion = f32[768,1024]{1,0:T(8,128)} fusion(bf16[2048,2048]{1,0:T(8,128)(2,1)} %all-gather.7.cloned.1.call-done, f32[2048]{0:T(1024)S(1)} %copy-done.6, f32[768]{0:T(1024)S(1)} %add_rsqrt_fusion.1, bf16[768,2048]{1,0:T(8,128)(2,1)} %all-reduce.2.cloned.1.call-done, bf16[768,2048]{1,0:T(8,128)(2,1)} %all-gather.5.cloned.1.call-done), kind=kOutput, calls=%fused_computation.5 | convolution fusion | flops 3230662656 | bytes 13642752 | tf_op jit(solution)/shard_map/dot_general | solution.py:92
  210.2 69.3 %all-gather.9.cloned.1.call-done = bf16[1024,2048]{0,1:T(8,128)(2,1)} async-done(((bf16[1024,64]{0,1:T(8,128)(2,1)}), bf16[1024,2048]{0,1:T(8,128)(2,1)}) %all-gather.9.cloned.1.call-update) | async-done | bytes 4194320 | tf_op jit(solution)/shard_map/all_gather | solution.py:95
  279.5 14.9 %convolution_convert_fusion = bf16[768,2048]{1,0:T(8,128)(2,1)} fusion(bf16[1024,2048]{0,1:T(8,128)(2,1)} %all-gather.9.cloned.1.call-done, f32[768,1024]{1,0:T(8,128)} %fusion, bf16[2048,2048]{1,0:T(8,128)(2,1)} %all-gather.7.cloned.1.call-done, f32[2048]{0:T(1024)S(1)} %copy-done.6, f32[768]{0:T(1024)S(1)} %add_rsqrt_fusion.1, ...), kind=kOutput, calls=%fused_computation.9 | convolution fusion | flops 6458179584 | bytes 20982784 | tf_op jit(solution)/shard_map/dot_general | solution.py:94
  294.4 3.7 %copy.23 = bf16[96,8,8,256]{3,2,0,1:T(8,128)(2,1)} copy(bf16[96,8,8,256]{3,2,1,0:T(8,128)(2,1)} %bitcast.58) | data formatting | bytes 6291456 | tf_op jit(solution)/shard_map/reshape | solution.py:41
  298.1 8.6 %all-to-all-start = ((bf16[8,768,256]{2,1,0:T(8,128)(2,1)}), bf16[8,768,256]{2,1,0:T(8,128)(2,1)}, u32[]{:S(2)}, u32[]{:S(2)}) async-start(bf16[8,768,256]{2,1,0:T(8,128)(2,1)} %bitcast.57), calls=%async_computation | async-start | bytes 6291456 | tf_op jit(solution)/shard_map/all_to_all | solution.py:47
  306.7 37.6 %all-to-all-done = bf16[8,768,256]{2,1,0:T(8,128)(2,1)} async-done(((bf16[8,768,256]{2,1,0:T(8,128)(2,1)}), bf16[8,768,256]{2,1,0:T(8,128)(2,1)}, u32[]{:S(2)}, u32[]{:S(2)}) %all-to-all-start) | async-done | bytes 3145760 | tf_op jit(solution)/shard_map/all_to_all | solution.py:47
  344.3 2.4 convert_reduce_fusion
  346.7 2.0 add_convert_fusion
  (27 shorter events, 1.4 us)
Async XLA Ops:
  7.4 83.3 %copy-start = (bf16[256,2048]{1,0:T(8,128)(2,1)S(1)}, bf16[256,2048]{1,0:T(8,128)(2,1)}, u32[]{:S(2)}) copy-start(bf16[256,2048]{1,0:T(8,128)(2,1)} %param.15) | copy-start | bytes 3145732
  7.4 40.5 %all-gather.5.cloned.1.call-start = ((), (), s32[]{:S(2)}) async-start(), calls=%async_computation.1 | async-start | bytes 3538944 | tf_op jit(solution)/shard_map/all_gather | solution.py:59
  8.1 166.7 %all-reduce.2.cloned.1.call-start = ((), (), s32[]{:S(2)}) async-start(), calls=%async_computation.2 | async-start | bytes 6291456 | tf_op jit(solution)/shard_map/psum | solution.py:85
  47.9 3.4 copy-start.1
  51.2 33.2 %copy-start.5 = (bf16[2048,256]{1,0:T(8,128)(2,1)S(1)}, bf16[2048,256]{1,0:T(8,128)(2,1)}, u32[]{:S(2)}) copy-start(bf16[2048,256]{1,0:T(8,128)(2,1)} %param.11) | copy-start | bytes 3145732
  85.6 0.7 copy-start.7
  87.6 2.9 copy-start.4
  93.4 0.9 copy-start.2
  93.4 1.0 copy-start.3
  93.4 107.5 %all-gather.7.cloned.1.call-start = ((), (), s32[]{:S(2)}) async-start(), calls=%async_computation.3 | async-start | bytes 8650752 | tf_op jit(solution)/shard_map/all_gather | solution.py:36
  95.1 184.4 %all-gather.9.cloned.1.call-start = ((), (), s32[]{:S(2)}) async-start(), calls=%async_computation.4 | async-start | bytes 4325376 | tf_op jit(solution)/shard_map/all_gather | solution.py:95
  95.7 105.2 %copy-start.6 = (f32[2048]{0:T(1024)S(1)}, f32[2048]{0:T(1024)}, u32[]{:S(2)}) copy-start(f32[2048]{0:T(1024)} %param.16) | copy-start | bytes 24580
  298.1 46.2 %all-to-all-start = ((bf16[8,768,256]{2,1,0:T(8,128)(2,1)}), bf16[8,768,256]{2,1,0:T(8,128)(2,1)}, u32[]{:S(2)}, u32[]{:S(2)}) async-start(bf16[8,768,256]{2,1,0:T(8,128)(2,1)} %bitcast.57), calls=%async_computation | async-start | bytes 6291456 | tf_op jit(solution)/shard_map/all_to_all | solution.py:47
Sparse Core Ops, SparseCore 0:
  10.0 37.8 all-gather.4
  93.5 81.2 all-reduce.1
Sparse Core Ops, SparseCore 1:
  96.5 104.4 all-gather.6
  203.4 76.1 all-gather.8
where the time goes:
time: 356 us
  waiting for transfers between devices  246 us (69%)
  matrix products  38.1 us (11%)
  blocking collectives  30.5 us (9%)
  between operations  15 us (4%)
  other arithmetic  12.2 us (3%)
  starting transfers between devices  8.92 us (3%)
  local copies, waits for them, and re-layouts  5.37 us (2%)
    psum x1, waiting for transfers between devices, body(): lax.psum(partial_value.astype(jnp.bfloat16), 'tp').astype(jnp.float32)  79.1 us
    all_gather x1, waiting for transfers between devices, body(): lax.all_gather(w_down, SEQ, axis=1, tiled=True)  69.3 us
    all_gather x1, waiting for transfers between devices, body(): features = lax.all_gather(tokens, 'tp', axis=1, tiled=True)  39.5 us
    all_to_all x1, waiting for transfers between devices, sum_at_owner(): lax.all_to_all(tiles, axis, split_axis=0, concat_axis=0, tiled=True)  37.6 us
    all_gather x2, blocking collectives, entering(): pieces = lax.all_gather(total.astype(jnp.bfloat16), axis)  30.5 us
    all_gather x1, waiting for transfers between devices, in_one_piece(): lax.all_gather(both, axis, axis=dim, tiled=True)  19.3 us
    dot_general x1, matrix products, body(): jnp.dot(hidden, lax.all_gather(w_down, SEQ, axis=1, tiled=True), preferre...  14.9 us
    dot_general x1, matrix products, body(): upward_sum = jnp.dot(ffn_in, pieces[1], preferred_element_type=jnp.float32)  9.24 us
  transfers between devices with their start and end apart: 5, of which 5 were waited for; matrix products, arithmetic and copies ran while one was open for 5% of the time, Pallas kernels for 0%

commit v1 on v0

--- a/solution.py
+++ b/solution.py
@@ -92,7 +92,9 @@
     upward_sum = jnp.dot(ffn_in, pieces[1], preferred_element_type=jnp.float32)
     hidden = (jax.nn.silu(gate_sum) * upward_sum).astype(jnp.bfloat16)
     terms = jnp.dot(
-        hidden, lax.all_gather(w_down, SEQ, axis=1, tiled=True), preferred_element_type=jnp.float32
+        hidden,
+        jnp.concatenate(lax.all_gather(w_down, SEQ), axis=1),
+        preferred_element_type=jnp.float32,
     )
     mlp_share = sum_at_owner(terms.astype(jnp.bfloat16), "tp", 1)
     return (resid + mlp_share).astype(jnp.bfloat16)

time: 356 us -> 366 us (1.028)
  local copies, waits for them, and re-layouts: 5.37 us -> 13.5 us
  waiting for transfers between devices: 246 us -> 250 us
    all_gather x1, waiting for transfers between devices: 19.3 us -> 91 us  [in_one_piece(): lax.all_gather(both, axis, axis=dim, tiled=True)]
    all_gather x1, waiting for transfers between devices: 69.3 us -> 0.6 us  [body(): lax.all_gather(w_down, SEQ)]
    reshape x0 -> x1, local copies, waits for them, and re-layouts: none -> 4.29 us  [body(): jnp.concatenate(lax.all_gather(w_down, SEQ), axis=1)]
    unnamed x16 -> x17, local copies, waits for them, and re-layouts: 1.65 us -> 5.55 us
  transfers between devices with their start and end apart: 5 -> 5, of which waited for: 5 -> 5; matrix products, arithmetic and copies ran while one was open for 5% -> 4% of each run, Pallas kernels for 0% -> 0%
where the time goes in v1:
time: 366 us; the launch traced here: 365 us
  waiting for transfers between devices  250 us (68%)
  matrix products  38.3 us (10%)
  blocking collectives  30.5 us (8%)
  between operations  15 us (4%)
  local copies, waits for them, and re-layouts  13.5 us (4%)
  other arithmetic  12.1 us (3%)
  starting transfers between devices  6.1 us (2%)
    all_gather x1, waiting for transfers between devices, in_one_piece(): lax.all_gather(both, axis, axis=dim, tiled=True)  91 us
    psum x1, waiting for transfers between devices, body(): lax.psum(partial_value.astype(jnp.bfloat16), 'tp').astype(jnp.float32)  79.8 us
    all_gather x1, waiting for transfers between devices, body(): features = lax.all_gather(tokens, 'tp', axis=1, tiled=True)  39.5 us
    all_to_all x1, waiting for transfers between devices, sum_at_owner(): lax.all_to_all(tiles, axis, split_axis=0, concat_axis=0, tiled=True)  37.6 us
    all_gather x2, blocking collectives, entering(): pieces = lax.all_gather(total.astype(jnp.bfloat16), axis)  30.5 us
    dot_general x1, matrix products, body(): jnp.dot(hidden, jnp.concatenate(lax.all_gather(w_down, SEQ), axis=1), pre...  15.1 us
    dot_general x1, matrix products, body(): upward_sum = jnp.dot(ffn_in, pieces[1], preferred_element_type=jnp.float32)  9.25 us
  transfers between devices with their start and end apart: 5, of which 5 were waited for; matrix products, arithmetic and copies ran while one was open for 4% of the time, Pallas kernels for 0%

profile of v1, /device:TPU:1, one launch (start us, length us, event | category | flops | bytes accessed | tf_op | source)
XLA Modules:
  0.0 365.2 jit_solution(699206692933125971)
XLA Ops:
  7.4 0.7 all-gather.6.cloned.1.call-update
  8.3 39.5 %all-gather.6.cloned.1.call-done = bf16[768,2048]{1,0:T(8,128)(2,1)} async-done(((bf16[768,256]{1,0:T(8,128)(2,1)}), bf16[768,2048]{1,0:T(8,128)(2,1)}) %all-gather.6.cloned.1.call-update) | async-done | bytes 3145744 | tf_op jit(solution)/shard_map/all_gather | solution.py:59
  47.9 3.3 convolution_convert_fusion.2
  51.2 2.4 convolution_convert_fusion.4
  53.9 20.8 %all-gather = bf16[16,128,128]{2,1,0:T(8,128)(2,1)S(1)} all-gather(bf16[2,128,128]{2,1,0:T(8,128)(2,1)S(1)} %convolution_convert_fusion.5), channel_id=2, replica_groups=mesh['seq_0'=4,'seq_1'=8,'tp'=8] {'seq_1'}, dimensions={0}, use_global_device_ids=true | all-gather | bytes 589824 | tf_op jit(solution)/shard_map/all_gather | solution.py:20
  74.7 9.7 %all_gather.25 = bf16[4,2,128,128]{3,2,1,0:T(8,128)(2,1)S(1)} all-gather(bf16[1,2,128,128]{3,2,1,0:T(8,128)(2,1)S(1)} %fusion.28), channel_id=1, replica_groups=mesh['seq_0'=4,'seq_1'=8,'tp'=8] {'seq_0'}, dimensions={0}, use_global_device_ids=true | all-gather | bytes 327680 | tf_op jit(solution)/shard_map/all_gather | solution.py:20
  84.5 1.1 convolution_convert_fusion.3
  85.6 0.7 copy-done.7
  86.3 1.3 fusion.29
  87.6 2.9 multiply_reduce_fusion.1
  90.6 2.7 convolution_convert_fusion.1
  94.3 0.7 pad_maximum_fusion
  95.1 79.8 %all-reduce.2.cloned.1.call-done = bf16[768,2048]{1,0:T(8,128)(2,1)} async-done(((bf16[768,2048]{1,0:T(8,128)(2,1)}), bf16[768,2048]{1,0:T(8,128)(2,1)}) %all-reduce.2.cloned.1.call-update) | async-done | bytes 3145744 | tf_op jit(solution)/shard_map/psum | solution.py:85
  174.9 6.6 %convert_add_fusion = (f32[768,2048]{1,0:T(8,128)}, f32[768]{0:T(1024)S(1)}) fusion(bf16[768,2048]{1,0:T(8,128)(2,1)} %all-reduce.2.cloned.1.call-done, bf16[768,2048]{1,0:T(8,128)(2,1)} %all-gather.6.cloned.1.call-done), kind=kLoop, calls=%fused_computation.3 | loop fusion | flops 7863552 | bytes 12585984 | tf_op jit(solution)/shard_map/add | solution.py:86
  182.0 4.6 %copy.36 = bf16[8,8,32,1024]{3,2,1,0:T(8,128)(2,1)S(1)} copy(bf16[8,8,32,1024]{3,1,2,0:T(8,128)(2,1)} %bitcast.66) | data formatting | bytes 8388608
  186.7 4.3 %copy.28 = bf16[1024,32,64]{0,2,1:T(8,128)(2,1)} copy(bf16[1024,32,64]{0,1,2:T(8,128)(2,1)S(1)} %bitcast.64) | data formatting | bytes 8388608 | tf_op jit(solution)/shard_map/reshape | solution.py:96
  191.0 91.0 %all-gather.8.cloned.1.call-done = bf16[2048,2048]{1,0:T(8,128)(2,1)} async-done(((bf16[64,2048]{1,0:T(8,128)(2,1)}), bf16[2048,2048]{1,0:T(8,128)(2,1)}) %all-gather.8.cloned.1.call-update) | async-done | bytes 8388624 | tf_op jit(solution)/shard_map/all_gather | solution.py:36
  281.9 9.2 %fusion = f32[768,1024]{1,0:T(8,128)} fusion(bf16[2048,2048]{1,0:T(8,128)(2,1)} %all-gather.8.cloned.1.call-done, f32[2048]{0:T(1024)S(1)} %copy-done.6, f32[768]{0:T(1024)S(1)} %add_rsqrt_fusion.1, bf16[768,2048]{1,0:T(8,128)(2,1)} %all-reduce.2.cloned.1.call-done, bf16[768,2048]{1,0:T(8,128)(2,1)} %all-gather.6.cloned.1.call-done), kind=kOutput, calls=%fused_computation.5 | convolution fusion | flops 3230662656 | bytes 13642752 | tf_op jit(solution)/shard_map/dot_general | solution.py:92
  291.2 15.1 %convolution_convert_fusion = bf16[768,2048]{1,0:T(8,128)(2,1)} fusion(bf16[1024,2048]{0,1:T(8,128)(2,1)} %bitcast.67, f32[768,1024]{1,0:T(8,128)} %fusion, bf16[2048,2048]{1,0:T(8,128)(2,1)} %all-gather.8.cloned.1.call-done, f32[2048]{0:T(1024)S(1)} %copy-done.6, f32[768]{0:T(1024)S(1)} %add_rsqrt_fusion.1, ...), kind=kOutput, calls=%fused_computation.9 | convolution fusion | flops 6458179584 | bytes 20982784 | tf_op jit(solution)/shard_map/dot_general | solution.py:94
  306.3 3.7 %copy.38 = bf16[96,8,8,256]{3,2,0,1:T(8,128)(2,1)} copy(bf16[96,8,8,256]{3,2,1,0:T(8,128)(2,1)} %bitcast.68) | data formatting | bytes 6291456 | tf_op jit(solution)/shard_map/reshape | solution.py:41
  310.0 5.8 %all-to-all-start = ((bf16[8,768,256]{2,1,0:T(8,128)(2,1)}), bf16[8,768,256]{2,1,0:T(8,128)(2,1)}, u32[]{:S(2)}, u32[]{:S(2)}) async-start(bf16[8,768,256]{2,1,0:T(8,128)(2,1)} %bitcast.65), calls=%async_computation | async-start | bytes 6291456 | tf_op jit(solution)/shard_map/all_to_all | solution.py:47
  315.8 37.6 %all-to-all-done = bf16[8,768,256]{2,1,0:T(8,128)(2,1)} async-done(((bf16[8,768,256]{2,1,0:T(8,128)(2,1)}), bf16[8,768,256]{2,1,0:T(8,128)(2,1)}, u32[]{:S(2)}, u32[]{:S(2)}) %all-to-all-start) | async-done | bytes 3145760 | tf_op jit(solution)/shard_map/all_to_all | solution.py:47
  353.3 2.4 convert_reduce_fusion
  355.7 2.0 add_convert_fusion
  (29 shorter events, 2.3 us)
Async XLA Ops:
  7.4 83.3 %copy-start = (bf16[256,2048]{1,0:T(8,128)(2,1)S(1)}, bf16[256,2048]{1,0:T(8,128)(2,1)}, u32[]{:S(2)}) copy-start(bf16[256,2048]{1,0:T(8,128)(2,1)} %param.15) | copy-start | bytes 3145732
  7.4 40.5 %all-gather.6.cloned.1.call-start = ((), (), s32[]{:S(2)}) async-start(), calls=%async_computation.1 | async-start | bytes 3538944 | tf_op jit(solution)/shard_map/all_gather | solution.py:59
  8.1 166.8 %all-reduce.2.cloned.1.call-start = ((), (), s32[]{:S(2)}) async-start(), calls=%async_computation.2 | async-start | bytes 6291456 | tf_op jit(solution)/shard_map/psum | solution.py:85
  47.9 3.4 copy-start.1
  51.2 33.2 %copy-start.5 = (bf16[2048,256]{1,0:T(8,128)(2,1)S(1)}, bf16[2048,256]{1,0:T(8,128)(2,1)}, u32[]{:S(2)}) copy-start(bf16[2048,256]{1,0:T(8,128)(2,1)} %param.11) | copy-start | bytes 3145732
  85.6 0.7 copy-start.7
  87.6 2.9 copy-start.4
  93.4 0.9 copy-start.2
  93.4 1.0 copy-start.3
  93.4 88.6 %all-gather.10.cloned.1.call-start = ((), (), s32[]{:S(2)}) async-start(), calls=%async_computation.4 | async-start | bytes 4325376 | tf_op jit(solution)/shard_map/all_gather | solution.py:96
  94.0 188.0 %all-gather.8.cloned.1.call-start = ((), (), s32[]{:S(2)}) async-start(), calls=%async_computation.3 | async-start | bytes 8650752 | tf_op jit(solution)/shard_map/all_gather | solution.py:36
  186.7 95.3 %copy-start.6 = (f32[2048]{0:T(1024)S(1)}, f32[2048]{0:T(1024)}, u32[]{:S(2)}) copy-start(f32[2048]{0:T(1024)} %param.16) | copy-start | bytes 24580
  310.0 43.4 %all-to-all-start = ((bf16[8,768,256]{2,1,0:T(8,128)(2,1)}), bf16[8,768,256]{2,1,0:T(8,128)(2,1)}, u32[]{:S(2)}, u32[]{:S(2)}) async-start(bf16[8,768,256]{2,1,0:T(8,128)(2,1)} %bitcast.65), calls=%async_computation | async-start | bytes 6291456 | tf_op jit(solution)/shard_map/all_to_all | solution.py:47
Sparse Core Ops, SparseCore 0:
  10.0 37.8 all-gather.5
  93.5 81.2 all-reduce.1
Sparse Core Ops, SparseCore 1:
  96.5 85.5 all-gather.9
  184.5 97.4 all-gather.7
